TPU v7x, 32 devices: a whole 2x2x4 slice. The times are simulated.
32 devices in a mesh: gx: 2 (over x), gy: 4 (over z), gz: 4 (over y, core).
Axes of the slice: x: 2, y: 2, z: 4, core: 2. Of those that a mesh axis runs over, the one named last changes fastest.
Arguments:
- velocity: float32 [3, 16, 32, 512], P(None, 'gx', 'gy', 'gz'), may hold values from -6 to 6
- direction: float32 [3, 16, 32, 512], P(None, 'gx', 'gy', 'gz'), may hold values from -3 to 3
- pressure: float32 [16, 32, 512], P('gx', 'gy', 'gz'), may hold values from -6 to 6
- body_force: float32 [3, 16, 32, 512], P(None, 'gx', 'gy', 'gz'), may hold values from -21 to 21, as said below
- phase_ids: int32 [16, 32, 512], P('gx', 'gy', 'gz'), may hold values from 0 to 3
- creep_factor: float32 [4], replicated, may hold values from 0.5 to 2
- stress_exponent: float32 [4], replicated, may hold values from 1.5 to 4
- yield_stress: float32 [4], replicated, may hold values from 0.5 to 3
- accepted: int32 [1], replicated, may hold values from 0 to 3
Outputs:
- norms: float32 [2, 4], replicated
- chosen_velocity: float32 [3, 16, 32, 512], P(None, 'gx', 'gy', 'gz')
- chosen_residual: float32 [3, 16, 32, 512], P(None, 'gx', 'gy', 'gz')
Inputs may be any that keep to these rules, and one draw needn't show every extreme that they name: `body_force`: body force on every cell and component.
All inputs are finite; a program needn't handle non-finite values.
Results may differ from a plain program's by a relative error of at most 0.00022.
Values sent between devices are 32-bit elements; how exact they have to be, the bound alone decides.
A program may use at most 64 MiB of HBM per device.

v0:
```python
import jax
import jax.numpy as jnp
from jax import lax
from jax.sharding import PartitionSpec as P

step_lengths = (1.0, 0.5, 0.25, 0.125)
rate_offset = 0.01
viscosity_least = 0.05
tiny_mean = 1e-06
tensor_slots = ((0, 3, 4), (3, 1, 5), (4, 5, 2))


def extended(array, sides, width):
    for axis, dim in sides:
        size, length = (lax.axis_size(axis), array.shape[dim])
        up = [(i, (i + 1) % size) for i in range(size - 1)]
        down = [(j, i) for i, j in up]
        last = lax.slice_in_dim(array, length - width, length, axis=dim)
        leading = lax.slice_in_dim(array, 0, width, axis=dim)
        before = lax.ppermute(last, axis, up)
        after = lax.ppermute(leading, axis, down)
        array = jnp.concatenate([before, array, after], axis=dim)
    return array


def centered(values, axis_number):
    lower = [slice(1, -1)] * 3
    upper = [slice(1, -1)] * 3
    lower[axis_number] = slice(0, -2)
    upper[axis_number] = slice(2, None)
    leading = (slice(None),) * (values.ndim - 3)
    return 0.5 * (values[leading + tuple(upper)] - values[leading + tuple(lower)])


def component(values, i):
    return lax.index_in_dim(values, i, values.ndim - 4, keepdims=False)


def strain_rates(padded):
    gradients = [[centered(component(padded, i), j) for j in range(3)] for i in range(3)]
    return jnp.stack(
        [
            gradients[0][0],
            gradients[1][1],
            gradients[2][2],
            0.5 * (gradients[0][1] + gradients[1][0]),
            0.5 * (gradients[0][2] + gradients[2][0]),
            0.5 * (gradients[1][2] + gradients[2][1]),
        ],
        axis=-4,
    )


def double_dot(first, second):
    diagonal = (
        component(first, 0) * component(second, 0)
        + component(first, 1) * component(second, 1)
        + component(first, 2) * component(second, 2)
    )
    offdiag = (
        component(first, 3) * component(second, 3)
        + component(first, 4) * component(second, 4)
        + component(first, 5) * component(second, 5)
    )
    return diagonal + 2.0 * offdiag


def effective_viscosity(rates, factor, exponent, yields):
    second = 0.5 * double_dot(rates, rates) + rate_offset
    creep_part = factor * jnp.power(second, (1.0 - exponent) / (2.0 * exponent))
    plastic = 0.5 * yields * lax.rsqrt(second)
    total_part = creep_part + plastic
    viscosity = creep_part * plastic / total_part + viscosity_least
    creep_slope = creep_part * (1.0 - exponent) / (2.0 * exponent * second)
    plastic_slope = -plastic / (2.0 * second)
    derivative = (plastic * plastic * creep_slope + creep_part * creep_part * plastic_slope) / (
        total_part * total_part
    )
    return (viscosity, derivative)


def spread_cells(values):
    return jnp.expand_dims(values, values.ndim - 3)


def divergence(padded):
    return jnp.stack(
        [
            centered(component(padded, tensor_slots[i][0]), 0)
            + centered(component(padded, tensor_slots[i][1]), 1)
            + centered(component(padded, tensor_slots[i][2]), 2)
            for i in range(3)
        ],
        axis=-4,
    )


def tangent_stress(viscosity, derivative, rates, change):
    return (
        2.0 * spread_cells(viscosity) * change
        + 2.0 * spread_cells(derivative * double_dot(rates, change)) * rates
    )


def phase_params(phase_ids, creep_factor, stress_exponent, yield_stress):
    choose = (
        phase_ids[None] == jnp.arange(creep_factor.shape[0], dtype=jnp.int32)[:, None, None, None]
    ).astype(jnp.float32)
    return tuple(
        (
            jnp.sum(choose * entries[:, None, None, None], axis=0)
            for entries in (creep_factor, stress_exponent, yield_stress)
        )
    )


def edge_mask(start, count, devices):
    spots = start * count - 1 + jnp.arange(count + 2, dtype=jnp.int32)
    return ((spots >= 0) & (spots < count * devices)).astype(jnp.float32)


def stress_stack(base_rates, change_rates, trial_rates, factor, exponent, yields):
    base_viscosity, base_slope = effective_viscosity(base_rates, factor, exponent, yields)
    trial_viscosity, unused_slope = effective_viscosity(trial_rates, factor, exponent, yields)
    base_stress = 2.0 * spread_cells(base_viscosity) * base_rates
    change_stress = tangent_stress(base_viscosity, base_slope, base_rates, change_rates)
    trial_stress = 2.0 * spread_cells(trial_viscosity) * trial_rates
    return jnp.concatenate([base_stress[None], change_stress[None], trial_stress], axis=0)


def body(
    velocity,
    direction,
    pressure,
    body_force,
    phase_ids,
    creep_factor,
    stress_exponent,
    yield_stress,
    accepted,
):
    padded_pressure = extended(pressure, (("gx", 0), ("gy", 1), ("gz", 2)), 1)
    loading = body_force - jnp.stack([centered(padded_pressure, j) for j in range(3)])
    paired = extended(jnp.stack([velocity, direction]), (("gx", 2), ("gy", 3), ("gz", 4)), 2)
    phase_wide = extended(phase_ids, (("gx", 0), ("gy", 1), ("gz", 2)), 2)
    wide_factor, wide_exponent, wide_yields = phase_params(
        phase_wide[1:-1, 1:-1, 1:-1], creep_factor, stress_exponent, yield_stress
    )
    trial_padded = jnp.stack([paired[0] + length * paired[1] for length in step_lengths])
    stresses = stress_stack(
        strain_rates(paired[0]),
        strain_rates(paired[1]),
        strain_rates(trial_padded),
        wide_factor,
        wide_exponent,
        wide_yields,
    )
    mask_x = edge_mask(lax.axis_index("gx"), velocity.shape[1], lax.axis_size("gx"))
    mask_y = edge_mask(lax.axis_index("gy"), velocity.shape[2], lax.axis_size("gy"))
    mask_z = edge_mask(lax.axis_index("gz"), velocity.shape[3], lax.axis_size("gz"))
    padded_stress = stresses * (
        mask_x[:, None, None] * mask_y[None, :, None] * mask_z[None, None, :]
    )
    divided = divergence(padded_stress)
    residual_base = divided[0] + loading
    jacobian = divided[1]
    trial_residuals = divided[2:] + loading[None]
    actual = []
    predicted = []
    chosen_velocity = jnp.zeros_like(velocity)
    chosen_residual = jnp.zeros_like(velocity)
    for number, length in enumerate(step_lengths):
        trial_residual = trial_residuals[number]
        linear = residual_base + length * jacobian
        actual.append(jnp.sum(trial_residual * trial_residual))
        predicted.append(jnp.sum(linear * linear))
        picked = accepted[0] == number
        chosen_velocity = jnp.where(picked, velocity + length * direction, chosen_velocity)
        chosen_residual = jnp.where(picked, trial_residual, chosen_residual)
    sums = lax.psum(jnp.stack(actual + predicted), ("gx", "gy", "gz"))
    cells = (
        3.0
        * velocity.shape[1]
        * velocity.shape[2]
        * velocity.shape[3]
        * lax.axis_size("gx")
        * lax.axis_size("gy")
        * lax.axis_size("gz")
    )
    norms = jnp.sqrt(sums / cells + tiny_mean).reshape(2, 4)
    return (norms, chosen_velocity, chosen_residual)


def solution(mesh):
    placed = (
        P(None, "gx", "gy", "gz"),
        P(None, "gx", "gy", "gz"),
        P("gx", "gy", "gz"),
        P(None, "gx", "gy", "gz"),
        P("gx", "gy", "gz"),
        P(),
        P(),
        P(),
        P(),
    )
    return jax.shard_map(
        body,
        mesh=mesh,
        in_specs=placed,
        out_specs=(P(), P(None, "gx", "gy", "gz"), P(None, "gx", "gy", "gz")),
        check_vma=False,
    )
```

profile of v0, /device:TPU:0, one launch (start us, length us, event | category | flops | bytes accessed | tf_op | source)
XLA Modules:
  0.0 138.5 jit_solution(3832466436431659568)
XLA Ops:
  0.7 0.9 pad_maximum_fusion.9
  1.6 4.9 %collective-permute-start.6 = (f32[2,3,2,8,128]{4,3,2,1,0:T(8,128)S(1)}, f32[2,3,2,8,128]{4,3,2,1,0:T(8,128)S(1)}, u32[]{:S(2)}, u32[]{:S(2)}) collective-permute-start(f32[2,3,2,8,128]{4,3,2,1,0:T(8,128)S(1)} %get-tuple-element.60), channel_id=1, source_target_pairs={{0,16},{1,17},{2,18},{3,19},{4,20},{5,21},{6,22},{7,23},{8,24},{9,... | collective-permute-start | bytes 147464 | tf_op jit(solution)/shard_map/ppermute | solution.py:20
  6.4 1.3 collective-permute-start.7
  7.7 0.7 fusion.70
  8.5 4.5 %collective-permute-start = (s32[2,8,128]{2,1,0:T(8,128)S(1)}, s32[2,8,128]{2,1,0:T(8,128)S(1)}, u32[]{:S(2)}, u32[]{:S(2)}) collective-permute-start(s32[2,8,128]{2,1,0:T(8,128)S(1)} %get-tuple-element.77), channel_id=1, source_target_pairs={{0,16},{1,17},{2,18},{3,19},{4,20},{5,21},{6,22},{7,23},{8,24},{9,... | collective-permute-start | bytes 24584 | tf_op jit(solution)/shard_map/ppermute | solution.py:20
  13.0 1.3 collective-permute-start.1
  14.3 0.7 fusion.69
  15.0 4.5 %collective-permute-start.13 = (f32[1,8,128]{2,1,0:T(8,128)S(1)}, f32[1,8,128]{2,1,0:T(8,128)S(1)}, u32[]{:S(2)}, u32[]{:S(2)}) collective-permute-start(f32[1,8,128]{2,1,0:T(8,128)S(1)} %get-tuple-element.75), channel_id=1, source_target_pairs={{0,16},{1,17},{2,18},{3,19},{4,20},{5,21},{6,22},{7,23},{8,24},{9,... | collective-permute-start | bytes 12296 | tf_op jit(solution)/shard_map/ppermute | solution.py:20
  20.4 0.4 collective-permute-done.13
  20.9 1.3 collective-permute-start.12
  22.2 4.2 %collective-permute-done.12 = f32[1,8,128]{2,1,0:T(8,128)S(1)} collective-permute-done((f32[1,8,128]{2,1,0:T(8,128)S(1)}, f32[1,8,128]{2,1,0:T(8,128)S(1)}, u32[]{:S(2)}, u32[]{:S(2)}) %collective-permute-start.12) | collective-permute-done | bytes 4128 | tf_op jit(solution)/shard_map/ppermute | solution.py:21
  26.3 0.9 fusion.51
  27.2 1.3 collective-permute-start.14
  28.6 4.5 %collective-permute-start.15 = (f32[10,1,128]{2,1,0:T(1,128)S(1)}, f32[10,1,128]{2,1,0:T(1,128)S(1)}, u32[]{:S(2)}, u32[]{:S(2)}) collective-permute-start(f32[10,1,128]{2,1,0:T(1,128)S(1)} %get-tuple-element.70), channel_id=1, source_target_pairs={{0,4},{4,8},{8,12},{1,5},{5,9},{9,13},{2,6},{6,10},{10,14},{3,7},{... | collective-permute-start | bytes 15368 | tf_op jit(solution)/shard_map/ppermute | solution.py:20
  33.1 0.8 constant_dynamic-update-slice_fusion.1
  33.9 3.5 %collective-permute-start.2 = (s32[12,2,128]{2,1,0:T(2,128)S(1)}, s32[12,2,128]{2,1,0:T(2,128)S(1)}, u32[]{:S(2)}, u32[]{:S(2)}) collective-permute-start(s32[12,2,128]{2,1,0:T(2,128)S(1)} %get-tuple-element.68), channel_id=1, source_target_pairs={{0,4},{4,8},{8,12},{1,5},{5,9},{9,13},{2,6},{6,10},{10,14},{3,7},{... | collective-permute-start | bytes 36872 | tf_op jit(solution)/shard_map/ppermute | solution.py:20
  37.4 1.3 collective-permute-start.3
  38.8 1.3 collective-permute-start.16
  40.1 3.0 %collective-permute-start.17 = (f32[10,10,1]{2,1,0:T(8,128)S(1)}, f32[10,10,1]{2,1,0:T(8,128)S(1)}, u32[]{:S(2)}, u32[]{:S(2)}) collective-permute-start(f32[10,10,1]{2,1,0:T(8,128)S(1)} %get-tuple-element.65), channel_id=1, source_target_pairs={{0,1},{1,2},{2,3},{4,5},{5,6},{6,7},{8,9},{9,10},{10,11},{12,13},{... | collective-permute-start | bytes 1208 | tf_op jit(solution)/shard_map/ppermute | solution.py:20
  43.3 3.0 %collective-permute-start.4 = (s32[12,12,2]{2,1,0:T(8,128)S(1)}, s32[12,12,2]{2,1,0:T(8,128)S(1)}, u32[]{:S(2)}, u32[]{:S(2)}) collective-permute-start(s32[12,12,2]{2,1,0:T(8,128)S(1)} %get-tuple-element.62), channel_id=1, source_target_pairs={{0,1},{1,2},{2,3},{4,5},{5,6},{6,7},{8,9},{9,10},{10,11},{12,13},{... | collective-permute-start | bytes 3464 | tf_op jit(solution)/shard_map/ppermute | solution.py:20
  46.4 1.3 collective-permute-start.5
  47.8 1.8 %collective-permute-done.5 = s32[12,12,2]{2,1,0:T(8,128)S(1)} collective-permute-done((s32[12,12,2]{2,1,0:T(8,128)S(1)}, s32[12,12,2]{2,1,0:T(8,128)S(1)}, u32[]{:S(2)}, u32[]{:S(2)}) %collective-permute-start.5) | collective-permute-done | bytes 1184 | tf_op jit(solution)/shard_map/ppermute | solution.py:21
  49.6 0.2 pad_add_fusion
  49.9 4.5 %collective-permute-start.8 = (f32[2,3,12,2,128]{4,3,2,1,0:T(2,128)S(1)}, f32[2,3,12,2,128]{4,3,2,1,0:T(2,128)S(1)}, u32[]{:S(2)}, u32[]{:S(2)}) collective-permute-start(f32[2,3,12,2,128]{4,3,2,1,0:T(2,128)S(1)} %get-tuple-element.58), channel_id=1, source_target_pairs={{0,4},{4,8},{8,12},{1,5},{5,9},{9,13},{2,6},{6,10},{10,14},{3,7},{... | collective-permute-start | bytes 221192 | tf_op jit(solution)/shard_map/ppermute | solution.py:20
  54.4 1.3 collective-permute-start.9
  55.8 0.9 select_reduce_fusion.2
  56.7 4.0 %collective-permute-done.9 = f32[2,3,12,2,128]{4,3,2,1,0:T(2,128)S(1)} collective-permute-done((f32[2,3,12,2,128]{4,3,2,1,0:T(2,128)S(1)}, f32[2,3,12,2,128]{4,3,2,1,0:T(2,128)S(1)}, u32[]{:S(2)}, u32[]{:S(2)}) %collective-permute-start.9) | collective-permute-done | bytes 73760 | tf_op jit(solution)/shard_map/ppermute | solution.py:21
  60.8 0.2 fusion.64
  61.0 0.5 copy.134
  61.6 3.7 %collective-permute-start.10 = (f32[2,3,12,12,2]{3,4,2,1,0:T(2,128)S(1)}, f32[2,3,12,12,2]{3,4,2,1,0:T(2,128)S(1)}, u32[]{:S(2)}, u32[]{:S(2)}) collective-permute-start(f32[2,3,12,12,2]{3,4,2,1,0:T(2,128)S(1)} %copy.134), channel_id=1, source_target_pairs={{0,1},{1,2},{2,3},{4,5},{5,6},{6,7},{8,9},{9,10},{10,11},{12,13},{... | collective-permute-start | bytes 20744 | tf_op jit(solution)/shard_map/ppermute | solution.py:20
  65.3 0.5 copy.135
  65.8 1.5 %collective-permute-start.11 = (f32[2,3,12,12,2]{3,4,2,1,0:T(2,128)S(1)}, f32[2,3,12,12,2]{3,4,2,1,0:T(2,128)S(1)}, u32[]{:S(2)}, u32[]{:S(2)}) collective-permute-start(f32[2,3,12,12,2]{3,4,2,1,0:T(2,128)S(1)} %copy.135), channel_id=1, source_target_pairs={{1,0},{2,1},{3,2},{5,4},{6,5},{7,6},{9,8},{10,9},{11,10},{13,12},{... | collective-permute-start | bytes 20744 | tf_op jit(solution)/shard_map/ppermute | solution.py:21
  67.4 0.6 copy.136
  67.9 1.9 %collective-permute-done.11 = f32[2,3,12,12,2]{3,4,2,1,0:T(2,128)S(1)} collective-permute-done((f32[2,3,12,12,2]{3,4,2,1,0:T(2,128)S(1)}, f32[2,3,12,12,2]{3,4,2,1,0:T(2,128)S(1)}, u32[]{:S(2)}, u32[]{:S(2)}) %collective-permute-start.11) | collective-permute-done | bytes 6944 | tf_op jit(solution)/shard_map/ppermute | solution.py:21
  69.8 0.6 copy.137
  70.4 0.8 pad_maximum_fusion.1
  71.3 0.3 slice_add_fusion
  71.6 0.2 fusion.40
  72.0 0.2 fusion.53
  72.2 0.8 add_multiply_fusion.1
  73.0 0.2 fusion.42
  73.3 0.5 copy.150
  73.8 0.5 copy.151
  74.3 0.5 copy.152
  74.7 0.5 copy.153
  75.2 1.8 %pad_maximum_fusion = f32[4,3,12,12,132]{4,0,3,2,1:T(4,128)S(1)} fusion(f32[1,3,12,12,132]{4,0,3,2,1:T(1,128)S(1)} %copy.153, f32[1,3,12,12,132]{4,0,3,2,1:T(1,128)S(1)} %copy.152, f32[1,3,12,12,132]{4,0,3,2,1:T(1,128)S(1)} %copy.151, f32[1,3,12,12,132]{4,0,3,2,1:T(1,128)S(1)} %copy.150), kind=kLoop, calls=%fused_computation.1 | loop fusion | flops 684288 | bytes 1824768 | tf_op jit(solution)/shard_map/stack | solution.py:149
  77.0 0.3 slice_bitcast_fusion.6
  77.3 0.5 bitcast_dynamic-update-slice_fusion.5
  77.8 0.1 copy_dynamic-update-slice_fusion.7
  78.1 1.1 multiply_multiply_fusion
  80.1 0.6 bitcast_dynamic-update-slice_fusion.4
  80.7 0.3 bitcast_dynamic-update-slice_fusion.3
  81.0 3.7 %add_multiply_fusion = (f32[4,10,10,130]{3,0,2,1:T(4,128)S(1)}, f32[4,10,10,130]{3,0,2,1:T(4,128)S(1)}, f32[4,10,10,130]{3,0,2,1:T(4,128)S(1)}, f32[4,10,10,130]{3,0,2,1:T(4,128)S(1)}) fusion(f32[10,10,130]{2,1,0:T(8,128)S(1)} %get-tuple-element.79, f32[10,10,130]{2,1,0:T(8,128)S(1)} %get-tuple-element.78, f32[10,10,130]{2,1,0:T(8,128)S(1)} %get-tuple-element.14, ...), kind=kLoop, calls=%fused_computation.43 | loop fusion | flops 2028000 | bytes 4732000 | tf_op jit(solution)/shard_map/mul | solution.py:127
  84.9 0.2 broadcast_multiply_fusion
  85.1 0.9 broadcast_multiply_fusion.1
  86.1 1.9 %maximum_multiply_fusion = f32[6,6,10,10,130]{4,0,3,2,1:T(8,128)S(1)} fusion(f32[4,6,10,10,130]{4,0,3,2,1:T(4,128)S(1)} %bitcast.105, f32[1,6,10,10,130]{4,0,3,2,1:T(1,128)S(1)} %get-tuple-element.54, f32[1,6,10,10,130]{4,0,3,2,1:T(1,128)S(1)} %get-tuple-element.53, f32[10,10,130]{2,1,0:T(8,128)S(1)} %broadcast_multiply_fusion.2), kind=kLoop, calls=%fused_computation | loop fusion | flops 1404000 | bytes 3796000 | tf_op jit(solution)/shard_map/mul | solution.py:161
  88.0 0.5 slice_bitcast_fusion
  88.5 1.1 fusion.11
  89.8 0.7 multiply_reduce_fusion
  90.5 1.3 multiply_reduce_fusion.4
  91.9 5.0 %stack.171 = f32[8]{0:T(128)S(1)} concatenate(f32[1]{0:T(128)} %bitcast.41, f32[1]{0:T(128)} %bitcast.42, f32[1]{0:T(128)} %bitcast.43, f32[1]{0:T(128)} %bitcast.44, f32[1]{0:T(128)} %bitcast.47, f32[1]{0:T(128)} %bitcast.48, f32[1]{0:T(128)} %bitcast.49, f32[1]{0:T(128)} %bitcast.50), dimensions={0} | concatenate | bytes 64 | tf_op jit(solution)/shard_map/stack | solution.py:180
  96.9 0.7 select_select_fusion
  97.6 40.2 %psum.7 = f32[8]{0:T(128)S(1)} all-reduce(f32[8]{0:T(128)S(1)} %stack.171), channel_id=1, replica_groups=mesh['gx'=2,'gy'=4,'gz'=4] {'gx','gy','gz'}, use_global_device_ids=true, to_apply=%region_11.12 | all-reduce | flops 8 | bytes 64 | tf_op jit(solution)/shard_map/psum | solution.py:180
  137.8 0.7 reshape.383
  (64 shorter events, 2.5 us)
Async XLA Ops:
  0.6 49.2 %copy-start.1 = (f32[3,8,8,128]{3,2,1,0:T(8,128)S(1)}, f32[3,8,8,128]{3,2,1,0:T(8,128)}, u32[]{:S(2)}) copy-start(f32[3,8,8,128]{3,2,1,0:T(8,128)} %param.9) | copy-start | bytes 294916
  0.6 49.2 %copy-start = (f32[3,8,8,128]{3,2,1,0:T(8,128)S(1)}, f32[3,8,8,128]{3,2,1,0:T(8,128)}, u32[]{:S(2)}) copy-start(f32[3,8,8,128]{3,2,1,0:T(8,128)} %param.10) | copy-start | bytes 294916
  0.7 55.1 %copy-start.3 = (f32[4]{0:T(128)S(1)}, f32[4]{0:T(128)}, u32[]{:S(2)}) copy-start(f32[4]{0:T(128)} %param.14) | copy-start | bytes 52
  0.7 55.1 %copy-start.5 = (f32[4]{0:T(128)S(1)}, f32[4]{0:T(128)}, u32[]{:S(2)}) copy-start(f32[4]{0:T(128)} %param.15) | copy-start | bytes 52
  0.7 55.1 %copy-start.4 = (f32[4]{0:T(128)S(1)}, f32[4]{0:T(128)}, u32[]{:S(2)}) copy-start(f32[4]{0:T(128)} %param.16) | copy-start | bytes 52
  1.6 48.2 %collective-permute-start.6 = (f32[2,3,2,8,128]{4,3,2,1,0:T(8,128)S(1)}, f32[2,3,2,8,128]{4,3,2,1,0:T(8,128)S(1)}, u32[]{:S(2)}, u32[]{:S(2)}) collective-permute-start(f32[2,3,2,8,128]{4,3,2,1,0:T(8,128)S(1)} %get-tuple-element.60), channel_id=1, source_target_pairs={{0,16},{1,17},{2,18},{3,19},{4,20},{5,21},{6,22},{7,23},{8,24},{9,... | collective-permute-start | bytes 147464 | tf_op jit(solution)/shard_map/ppermute | solution.py:20
  6.4 43.4 %collective-permute-start.7 = (f32[2,3,2,8,128]{4,3,2,1,0:T(8,128)S(1)}, f32[2,3,2,8,128]{4,3,2,1,0:T(8,128)S(1)}, u32[]{:S(2)}, u32[]{:S(2)}) collective-permute-start(f32[2,3,2,8,128]{4,3,2,1,0:T(8,128)S(1)} %get-tuple-element.61), channel_id=1, source_target_pairs={{16,0},{17,1},{18,2},{19,3},{20,4},{21,5},{22,6},{23,7},{24,8},{25... | collective-permute-start | bytes 147464 | tf_op jit(solution)/shard_map/ppermute | solution.py:21
  8.5 20.1 %collective-permute-start = (s32[2,8,128]{2,1,0:T(8,128)S(1)}, s32[2,8,128]{2,1,0:T(8,128)S(1)}, u32[]{:S(2)}, u32[]{:S(2)}) collective-permute-start(s32[2,8,128]{2,1,0:T(8,128)S(1)} %get-tuple-element.77), channel_id=1, source_target_pairs={{0,16},{1,17},{2,18},{3,19},{4,20},{5,21},{6,22},{7,23},{8,24},{9,... | collective-permute-start | bytes 24584 | tf_op jit(solution)/shard_map/ppermute | solution.py:20
  13.0 20.9 %collective-permute-start.1 = (s32[2,8,128]{2,1,0:T(8,128)S(1)}, s32[2,8,128]{2,1,0:T(8,128)S(1)}, u32[]{:S(2)}, u32[]{:S(2)}) collective-permute-start(s32[2,8,128]{2,1,0:T(8,128)S(1)} %get-tuple-element.76), channel_id=1, source_target_pairs={{16,0},{17,1},{18,2},{19,3},{20,4},{21,5},{22,6},{23,7},{24,8},{25... | collective-permute-start | bytes 24584 | tf_op jit(solution)/shard_map/ppermute | solution.py:21
  15.0 5.8 %collective-permute-start.13 = (f32[1,8,128]{2,1,0:T(8,128)S(1)}, f32[1,8,128]{2,1,0:T(8,128)S(1)}, u32[]{:S(2)}, u32[]{:S(2)}) collective-permute-start(f32[1,8,128]{2,1,0:T(8,128)S(1)} %get-tuple-element.75), channel_id=1, source_target_pairs={{0,16},{1,17},{2,18},{3,19},{4,20},{5,21},{6,22},{7,23},{8,24},{9,... | collective-permute-start | bytes 12296 | tf_op jit(solution)/shard_map/ppermute | solution.py:20
  20.9 5.5 %collective-permute-start.12 = (f32[1,8,128]{2,1,0:T(8,128)S(1)}, f32[1,8,128]{2,1,0:T(8,128)S(1)}, u32[]{:S(2)}, u32[]{:S(2)}) collective-permute-start(f32[1,8,128]{2,1,0:T(8,128)S(1)} %get-tuple-element.74), channel_id=1, source_target_pairs={{16,0},{17,1},{18,2},{19,3},{20,4},{21,5},{22,6},{23,7},{24,8},{25... | collective-permute-start | bytes 12296 | tf_op jit(solution)/shard_map/ppermute | solution.py:21
  27.2 10.2 %collective-permute-start.14 = (f32[10,1,128]{2,1,0:T(1,128)S(1)}, f32[10,1,128]{2,1,0:T(1,128)S(1)}, u32[]{:S(2)}, u32[]{:S(2)}) collective-permute-start(f32[10,1,128]{2,1,0:T(1,128)S(1)} %get-tuple-element.71), channel_id=1, source_target_pairs={{4,0},{8,4},{12,8},{5,1},{9,5},{13,9},{6,2},{10,6},{14,10},{7,3},{... | collective-permute-start | bytes 15368 | tf_op jit(solution)/shard_map/ppermute | solution.py:21
  28.6 10.2 %collective-permute-start.15 = (f32[10,1,128]{2,1,0:T(1,128)S(1)}, f32[10,1,128]{2,1,0:T(1,128)S(1)}, u32[]{:S(2)}, u32[]{:S(2)}) collective-permute-start(f32[10,1,128]{2,1,0:T(1,128)S(1)} %get-tuple-element.70), channel_id=1, source_target_pairs={{0,4},{4,8},{8,12},{1,5},{5,9},{9,13},{2,6},{6,10},{10,14},{3,7},{... | collective-permute-start | bytes 15368 | tf_op jit(solution)/shard_map/ppermute | solution.py:20
  33.9 6.2 %collective-permute-start.2 = (s32[12,2,128]{2,1,0:T(2,128)S(1)}, s32[12,2,128]{2,1,0:T(2,128)S(1)}, u32[]{:S(2)}, u32[]{:S(2)}) collective-permute-start(s32[12,2,128]{2,1,0:T(2,128)S(1)} %get-tuple-element.68), channel_id=1, source_target_pairs={{0,4},{4,8},{8,12},{1,5},{5,9},{9,13},{2,6},{6,10},{10,14},{3,7},{... | collective-permute-start | bytes 36872 | tf_op jit(solution)/shard_map/ppermute | solution.py:20
  37.4 5.8 %collective-permute-start.3 = (s32[12,2,128]{2,1,0:T(2,128)S(1)}, s32[12,2,128]{2,1,0:T(2,128)S(1)}, u32[]{:S(2)}, u32[]{:S(2)}) collective-permute-start(s32[12,2,128]{2,1,0:T(2,128)S(1)} %get-tuple-element.69), channel_id=1, source_target_pairs={{4,0},{8,4},{12,8},{5,1},{9,5},{13,9},{6,2},{10,6},{14,10},{7,3},{... | collective-permute-start | bytes 36872 | tf_op jit(solution)/shard_map/ppermute | solution.py:21
  38.8 7.5 %collective-permute-start.16 = (f32[10,10,1]{2,1,0:T(8,128)S(1)}, f32[10,10,1]{2,1,0:T(8,128)S(1)}, u32[]{:S(2)}, u32[]{:S(2)}) collective-permute-start(f32[10,10,1]{2,1,0:T(8,128)S(1)} %get-tuple-element.64), channel_id=1, source_target_pairs={{1,0},{2,1},{3,2},{5,4},{6,5},{7,6},{9,8},{10,9},{11,10},{13,12},{... | collective-permute-start | bytes 1208 | tf_op jit(solution)/shard_map/ppermute | solution.py:21
  40.1 7.5 %collective-permute-start.17 = (f32[10,10,1]{2,1,0:T(8,128)S(1)}, f32[10,10,1]{2,1,0:T(8,128)S(1)}, u32[]{:S(2)}, u32[]{:S(2)}) collective-permute-start(f32[10,10,1]{2,1,0:T(8,128)S(1)} %get-tuple-element.65), channel_id=1, source_target_pairs={{0,1},{1,2},{2,3},{4,5},{5,6},{6,7},{8,9},{9,10},{10,11},{12,13},{... | collective-permute-start | bytes 1208 | tf_op jit(solution)/shard_map/ppermute | solution.py:20
  43.3 4.5 %collective-permute-start.4 = (s32[12,12,2]{2,1,0:T(8,128)S(1)}, s32[12,12,2]{2,1,0:T(8,128)S(1)}, u32[]{:S(2)}, u32[]{:S(2)}) collective-permute-start(s32[12,12,2]{2,1,0:T(8,128)S(1)} %get-tuple-element.62), channel_id=1, source_target_pairs={{0,1},{1,2},{2,3},{4,5},{5,6},{6,7},{8,9},{9,10},{10,11},{12,13},{... | collective-permute-start | bytes 3464 | tf_op jit(solution)/shard_map/ppermute | solution.py:20
  46.4 3.2 %collective-permute-start.5 = (s32[12,12,2]{2,1,0:T(8,128)S(1)}, s32[12,12,2]{2,1,0:T(8,128)S(1)}, u32[]{:S(2)}, u32[]{:S(2)}) collective-permute-start(s32[12,12,2]{2,1,0:T(8,128)S(1)} %get-tuple-element.63), channel_id=1, source_target_pairs={{1,0},{2,1},{3,2},{5,4},{6,5},{7,6},{9,8},{10,9},{11,10},{13,12},{... | collective-permute-start | bytes 3464 | tf_op jit(solution)/shard_map/ppermute | solution.py:21
  49.9 6.8 %collective-permute-start.8 = (f32[2,3,12,2,128]{4,3,2,1,0:T(2,128)S(1)}, f32[2,3,12,2,128]{4,3,2,1,0:T(2,128)S(1)}, u32[]{:S(2)}, u32[]{:S(2)}) collective-permute-start(f32[2,3,12,2,128]{4,3,2,1,0:T(2,128)S(1)} %get-tuple-element.58), channel_id=1, source_target_pairs={{0,4},{4,8},{8,12},{1,5},{5,9},{9,13},{2,6},{6,10},{10,14},{3,7},{... | collective-permute-start | bytes 221192 | tf_op jit(solution)/shard_map/ppermute | solution.py:20
  54.4 6.2 %collective-permute-start.9 = (f32[2,3,12,2,128]{4,3,2,1,0:T(2,128)S(1)}, f32[2,3,12,2,128]{4,3,2,1,0:T(2,128)S(1)}, u32[]{:S(2)}, u32[]{:S(2)}) collective-permute-start(f32[2,3,12,2,128]{4,3,2,1,0:T(2,128)S(1)} %get-tuple-element.59), channel_id=1, source_target_pairs={{4,0},{8,4},{12,8},{5,1},{9,5},{13,9},{6,2},{10,6},{14,10},{7,3},{... | collective-permute-start | bytes 221192 | tf_op jit(solution)/shard_map/ppermute | solution.py:21
  61.6 5.8 %collective-permute-start.10 = (f32[2,3,12,12,2]{3,4,2,1,0:T(2,128)S(1)}, f32[2,3,12,12,2]{3,4,2,1,0:T(2,128)S(1)}, u32[]{:S(2)}, u32[]{:S(2)}) collective-permute-start(f32[2,3,12,12,2]{3,4,2,1,0:T(2,128)S(1)} %copy.134), channel_id=1, source_target_pairs={{0,1},{1,2},{2,3},{4,5},{5,6},{6,7},{8,9},{9,10},{10,11},{12,13},{... | collective-permute-start | bytes 20744 | tf_op jit(solution)/shard_map/ppermute | solution.py:20
  65.8 4.0 %collective-permute-start.11 = (f32[2,3,12,12,2]{3,4,2,1,0:T(2,128)S(1)}, f32[2,3,12,12,2]{3,4,2,1,0:T(2,128)S(1)}, u32[]{:S(2)}, u32[]{:S(2)}) collective-permute-start(f32[2,3,12,12,2]{3,4,2,1,0:T(2,128)S(1)} %copy.135), channel_id=1, source_target_pairs={{1,0},{2,1},{3,2},{5,4},{6,5},{7,6},{9,8},{10,9},{11,10},{13,12},{... | collective-permute-start | bytes 20744 | tf_op jit(solution)/shard_map/ppermute | solution.py:21
  88.5 1.2 copy-start.2
where the time goes:
time: 139 us; the launch traced here: 138 us
  starting transfers between devices  48.1 us (35%)
  blocking collectives  40.2 us (29%)
  other arithmetic  20.8 us (15%)
  local copies, waits for them, and re-layouts  15 us (11%)
  waiting for transfers between devices  12.4 us (9%)
  between operations  1.97 us (1%)
    psum x1, blocking collectives, body(): sums = lax.psum(jnp.stack(actual + predicted), ('gx', 'gy', 'gz'))  40.2 us
    ppermute x9, starting transfers between devices, extended(): before = lax.ppermute(last, axis, up)  36.3 us
    ppermute x9, waiting for transfers between devices, extended(): after = lax.ppermute(leading, axis, down)  11.9 us
    ppermute x9, starting transfers between devices, extended(): after = lax.ppermute(leading, axis, down)  11.8 us
    another operation x1, local copies, waits for them, and re-layouts, body(): sums = lax.psum(jnp.stack(actual + predicted), ('gx', 'gy', 'gz'))  5.04 us
    mul x2, other arithmetic, stress_stack(): trial_stress = 2.0 * spread_cells(trial_viscosity) * trial_rates  3.93 us
  transfers between devices with their start and end apart: 18, of which 5 were waited for; matrix products, arithmetic and copies ran while one was open for 4% of the time, Pallas kernels for 0%

commit v1 on v0

v1 whole, which is shorter than its diff:
```python
import functools

import jax
import jax.numpy as jnp
from jax import lax
from jax.experimental import pallas as pl
from jax.experimental.pallas import tpu as pltpu
from jax.sharding import PartitionSpec as P

step_lengths = (1.0, 0.5, 0.25, 0.125)
rate_offset = 0.01
viscosity_least = 0.05
tiny_mean = 1e-06
MESH = pl.DeviceIdType.MESH
AXES = ("gx", "gy", "gz")
INV_LN2 = 1.4426950408889634
FACE_COMPONENTS = ((0, 3, 4), (3, 1, 5), (4, 5, 2))


def spin(values, shift, axis):
    return pltpu.roll(values, shift % values.shape[axis], axis)


def offsets():
    found = []
    for dx in (-1, 0, 1):
        for dy in (-1, 0, 1):
            for dz in (-1, 0, 1):
                if 1 <= abs(dx) + abs(dy) + abs(dz) <= 2:
                    found.append((dx, dy, dz))
    return sorted(found, key=lambda o: (o[2] != 0, sum(map(abs, o))))


def stress_fields(E, F, phase, params, components, mask):
    factors, powers, yields = params
    factor, power, half_yield = factors[-1], powers[-1], yields[-1]
    for k in range(len(factors) - 2, -1, -1):
        here = phase == float(k)
        factor = jnp.where(here, factors[k], factor)
        power = jnp.where(here, powers[k], power)
        half_yield = jnp.where(here, yields[k], half_yield)

    def dot(a, b):
        diagonal = a[0] * b[0] + a[1] * b[1] + a[2] * b[2]
        return diagonal + 2.0 * (a[3] * b[3] + a[4] * b[4] + a[5] * b[5])

    def parts(rates):
        second = 0.125 * dot(rates, rates) + rate_offset
        creep = factor * jnp.exp2(power * jnp.log(second))
        plastic = half_yield * lax.rsqrt(second)
        total = creep + plastic
        inverse = 1.0 / total
        return second, creep, plastic, inverse, creep * plastic * inverse

    second, creep, plastic, inverse, mixed = parts(E)
    half = 0.5 * mixed + 0.5 * viscosity_least
    slope = mixed * (plastic * (power * (1.0 / INV_LN2)) - 0.5 * creep) * inverse / second
    coupling = 0.125 * slope * dot(E, F)
    if mask is not None:
        half = half * mask
        coupling = coupling * mask
    fields = [[half * E[i] for i in components]]
    fields.append([half * F[i] + coupling * E[i] for i in components])
    for length in step_lengths:
        rates = [e + length * f if length != 1.0 else e + f for e, f in zip(E, F)]
        half = 0.5 * parts(rates)[4] + 0.5 * viscosity_least
        if mask is not None:
            half = half * mask
        fields.append([half * rates[i] for i in components])
    return fields


def twice_rates(g):
    return [
        g[0][0],
        g[1][1],
        g[2][2],
        0.5 * (g[0][1] + g[1][0]),
        0.5 * (g[0][2] + g[2][0]),
        0.5 * (g[1][2] + g[2][1]),
    ]


def kernel(
    sizes,
    creep_ref, exponent_ref, yield_ref, accepted_ref,
    v_ref, d_ref, p_ref, b_ref, m_ref,
    norms_ref, cv_ref, cr_ref,
    sx, sy, sxy, sz,
    rx, ry, rz, rxy, rxz, ryz,
    own, xs_ref, ys_ref, red,
    send_sem, recv_sem, red_send, red_recv,
):
    nx, ny, nz = v_ref.shape[1:]
    me = [lax.axis_index(a) for a in AXES]
    offs = offsets()

    def exists(o):
        ok = None
        for k in range(3):
            if o[k]:
                here = me[k] > 0 if o[k] < 0 else me[k] < sizes[k] - 1
                ok = here if ok is None else jnp.logical_and(ok, here)
        return ok

    def device(o):
        return tuple(me[k] + o[k] for k in range(3))

    def mate(axis, off):
        place = list(me)
        place[axis] = lax.rem(me[axis] + off, sizes[axis])
        return tuple(place)

    barrier = pltpu.get_barrier_semaphore()
    count = sum(n - 1 for n in sizes)
    for o in offs:
        @pl.when(exists(o))
        def _():
            pl.semaphore_signal(barrier, inc=1, device_id=device(o), device_id_type=MESH)
        count = count + exists(o).astype(jnp.int32)
    for axis in range(3):
        for off in range(1, sizes[axis]):
            pl.semaphore_signal(barrier, inc=1, device_id=mate(axis, off), device_id_type=MESH)

    sub = lax.broadcasted_iota(jnp.int32, (ny, nz), 0)
    lane = lax.broadcasted_iota(jnp.int32, (ny, nz), 1)
    quad = lane % 4
    first, last = lane == 0, lane == nz - 1
    top, bottom = sub == 0, sub == ny - 1
    is_left = quad < 2

    def vel(c, x):
        return v_ref[c, x] if c < 3 else d_ref[c - 3, x]

    def entity(e, x):
        if e < 6:
            return vel(e, x)
        return p_ref[x] if e == 6 else m_ref[x].astype(jnp.float32)

    for s in range(2):
        near, far = (0, 1) if s == 0 else (nx - 1, nx - 2)
        for c in range(6):
            sx[s, 2 * c] = vel(c, near)
            sx[s, 2 * c + 1] = vel(c, far)
        sx[s, 12] = p_ref[near]
        sx[s, 13] = m_ref[near].astype(jnp.float32)
        near, far = (0, 1) if s == 0 else (ny - 1, ny - 2)
        edge = jnp.zeros((nx, nz), jnp.float32)
        for c in range(6):
            source = v_ref if c < 3 else d_ref
            plane = source[c % 3, :, near, :]
            sy[s, 2 * c] = plane
            sy[s, 2 * c + 1] = source[c % 3, :, far, :]
            edge = jnp.where(lane // 2 == c, spin(plane, 2 * c + 1, 1), edge)
            for side in range(2):
                x = 0 if side == 0 else nx - 1
                sxy[side, s, pl.ds(c, 1), :] = source[c % 3, x, pl.ds(near, 1), :]
        sy[s, 12] = p_ref[:, near, :]
        sy[s, 13] = m_ref[:, near, :].astype(jnp.float32)
        sz[s, 2] = edge
    for half in range(2):
        pack = jnp.zeros((ny, nz), jnp.float32)
        for e in range(4):
            for x in range(nx):
                base = 4 * (e * nx + x)
                pack = jnp.where(lane // 4 == base // 4, spin(entity(4 * half + e, x), base + 2, 1), pack)
        sz[0, half] = pack
        sz[1, half] = pack

    def ends(o):
        side = [(k + 1) // 2 for k in o]
        back = [1 - k for k in side]
        dx, dy, dz = o
        if dx and dy:
            return sxy.at[side[0], side[1]], rxy.at[back[0], back[1]]
        if dx and dz:
            return sz.at[0, pl.ds(0, 2)], rxz.at[back[0], back[2]]
        if dy and dz:
            return sz.at[side[1]], ryz.at[back[1], back[2]]
        if dx:
            return sx.at[side[0]], rx.at[back[0]]
        if dy:
            return sy.at[side[1]], ry.at[back[1]]
        return sz.at[0, pl.ds(0, 2)], rz.at[back[2]]

    def copy_of(o):
        source, target = ends(o)
        mirror = tuple(-k for k in o)
        return pltpu.make_async_remote_copy(
            src_ref=source, dst_ref=target,
            send_sem=send_sem.at[offs.index(o)], recv_sem=recv_sem.at[offs.index(mirror)],
            device_id=device(o), device_id_type=MESH,
        )

    pl.semaphore_wait(barrier, count)
    for o in offs:
        @pl.when(exists(o))
        def _():
            copy_of(o).start()

    lengths = jnp.float32(step_lengths[-1])
    accepted = accepted_ref[0]
    for k in range(len(step_lengths) - 2, -1, -1):
        lengths = jnp.where(accepted == k, jnp.float32(step_lengths[k]), lengths)
    for c in range(3):
        for x in range(nx):
            cv_ref[c, x] = v_ref[c, x] + lengths * d_ref[c, x]

    phases = creep_ref.shape[0]
    full = lambda value: jnp.full((ny, nz), value, jnp.float32)
    factors = [full(creep_ref[k]) for k in range(phases)]
    halves = [0.5 * full(yield_ref[k]) for k in range(phases)]
    powers = []
    for k in range(phases):
        n = full(exponent_ref[k])
        powers.append((1.0 - n) / (2.0 * n) * INV_LN2)
    params = (factors, powers, halves)

    for o in offs:
        mirror = tuple(-k for k in o)
        _, target = ends(mirror)

        @pl.when(exists(o))
        def _():
            copy_of(mirror).wait_recv()

        @pl.when(jnp.logical_not(exists(o)))
        def _():
            target[...] = jnp.zeros(target.shape, jnp.float32)

    def along_y(V, before, after):
        down = spin(jnp.where(bottom, before, V), 1, 0)
        up = spin(jnp.where(top, after, V), -1, 0)
        return up - down

    def along_z(V, T):
        down = spin(jnp.where(last, T, V), 1, 1)
        up = spin(jnp.where(first, T, V), -1, 1)
        return up - down

    def scale_of(o):
        return jnp.full((ny, nz), exists(o).astype(jnp.float32))

    W = [jnp.where(is_left, rz[0, h], rz[1, h]) for h in range(2)]
    XW = [[jnp.where(is_left, rxz[s, 0, h], rxz[s, 1, h]) for h in range(2)] for s in range(2)]
    YW = [[jnp.where(is_left, ryz[s, 0, h], ryz[s, 1, h]) for h in range(2)] for s in range(2)]
    YE = [jnp.where(lane % 2 == 0, ryz[s, 0, 2], ryz[s, 1, 2]) for s in range(2)]

    def quad_at(packed, e, x):
        return spin(packed[e // 4], -(4 * ((e % 4) * nx + x) + 2), 1)

    for s in range(2):
        x = 0 if s == 0 else nx - 1
        g = []
        for c in range(6):
            B, A, O = rx[s, 2 * c], rx[s, 2 * c + 1], vel(c, x)
            dx = O - A if s == 0 else A - O
            dy = along_y(B, rxy[s, 0, pl.ds(c, 1), :], rxy[s, 1, pl.ds(c, 1), :])
            dz = along_z(B, quad_at(XW[s], c, nx - 1 - x))
            g.append((dx, dy, dz))
        fields = stress_fields(
            twice_rates(g[:3]), twice_rates(g[3:]), rx[s, 13], params,
            FACE_COMPONENTS[0], scale_of((2 * s - 1, 0, 0)),
        )
        for f in range(6):
            for i in range(3):
                xs_ref[s, 3 * f + i] = fields[f][i]

    for s in range(2):
        g = []
        for c in range(6):
            B, A, O = ry[s, 2 * c], ry[s, 2 * c + 1], sy[s, 2 * c]
            dy = O - A if s == 0 else A - O
            dx = along_y(B, rxy[0, s, pl.ds(c, 1), :], rxy[1, s, pl.ds(c, 1), :])
            dz = along_z(B, spin(YE[s], -(2 * c + 1), 1))
            g.append((dx, dy, dz))
        fields = stress_fields(
            twice_rates(g[:3]), twice_rates(g[3:]), ry[s, 13], params,
            FACE_COMPONENTS[1], scale_of((0, 2 * s - 1, 0)),
        )
        for f in range(6):
            for i in range(3):
                ys_ref[s, 3 * f + i] = fields[f][i]

    spot = (lane // 4) % nx
    packed = []
    for h in range(2):
        O = sz[0, h]
        dz = jnp.where(
            quad == 1,
            spin(O, -1, 1) - spin(W[h], 1, 1),
            spin(W[h], -1, 1) - spin(O, 1, 1),
        )
        turn = 4 * (nx - 1)
        down = jnp.where(spot == 0, spin(XW[0][h], -turn, 1), spin(W[h], 4, 1))
        up = jnp.where(spot == nx - 1, spin(XW[1][h], turn, 1), spin(W[h], -4, 1))
        dy = along_y(W[h], YW[0][h], YW[1][h])
        packed.append((up - down, dy, dz))
    g = []
    for c in range(6):
        g.append([spin(packed[c // 4][j], -4 * nx * (c % 4), 1) for j in range(3)])
    inside = jnp.where(
        quad == 1, scale_of((0, 0, -1)), jnp.where(quad == 2, scale_of((0, 0, 1)), 0.0)
    )
    z_fields = stress_fields(
        twice_rates(g[:3]), twice_rates(g[3:]), spin(W[1], -4 * nx * 3, 1), params,
        FACE_COMPONENTS[2], inside,
    )

    for x in range(nx):
        g = []
        for c in range(6):
            V = vel(c, x)
            after = vel(c, x + 1) if x < nx - 1 else rx[1, 2 * c]
            before = vel(c, x - 1) if x > 0 else rx[0, 2 * c]
            dy = along_y(V, ry[0, 2 * c, pl.ds(x, 1), :], ry[1, 2 * c, pl.ds(x, 1), :])
            g.append((after - before, dy, along_z(V, quad_at(W, c, x))))
        fields = stress_fields(
            twice_rates(g[:3]), twice_rates(g[3:]), m_ref[x].astype(jnp.float32), params,
            range(6), None,
        )
        for f in range(6):
            for i in range(6):
                own[6 * f + i, x] = fields[f][i]

    sums = [jnp.zeros((ny, nz), jnp.float32) for _ in range(8)]
    for x in range(nx):
        pressure = p_ref[x]
        after = p_ref[x + 1] if x < nx - 1 else rx[1, 12]
        before = p_ref[x - 1] if x > 0 else rx[0, 12]
        slopes = (
            after - before,
            along_y(pressure, ry[0, 12, pl.ds(x, 1), :], ry[1, 12, pl.ds(x, 1), :]),
            along_z(pressure, quad_at(W, 6, x)),
        )
        for i in range(3):
            a, b, c = (FACE_COMPONENTS[j][i] for j in range(3))
            loading = b_ref[i, x] - 0.5 * slopes[i]
            divided = []
            for f in range(6):
                after = own[6 * f + a, x + 1] if x < nx - 1 else xs_ref[1, 3 * f + i]
                before = own[6 * f + a, x - 1] if x > 0 else xs_ref[0, 3 * f + i]
                dy = along_y(
                    own[6 * f + b, x],
                    ys_ref[0, 3 * f + i, pl.ds(x, 1), :],
                    ys_ref[1, 3 * f + i, pl.ds(x, 1), :],
                )
                dz = along_z(own[6 * f + c, x], spin(z_fields[f][i], -(4 * x + 2), 1))
                divided.append((after - before) + dy + dz)
            base = divided[0] + loading
            chosen = None
            for k in range(3, -1, -1):
                residual = divided[2 + k] + loading
                linear = base + step_lengths[k] * divided[1]
                sums[k] = sums[k] + residual * residual
                sums[4 + k] = sums[4 + k] + linear * linear
                chosen = residual if chosen is None else jnp.where(accepted == k, residual, chosen)
            cr_ref[i, x] = chosen

    total = jnp.zeros((ny, nz), jnp.float32)
    for k in range(8):
        total = jnp.where(sub == k, jnp.sum(sums[k], axis=0, keepdims=True), total)
    start = 0
    for axis in (2, 1, 0):
        n = sizes[axis]
        red[start + me[axis]] = total

        def share(off, incoming):
            other = lax.rem(me[axis] + off, n)
            slot = start + (other if incoming else me[axis])
            return pltpu.make_async_remote_copy(
                src_ref=red.at[start + me[axis]], dst_ref=red.at[slot],
                send_sem=red_send.at[start + off], recv_sem=red_recv.at[slot],
                device_id=mate(axis, off), device_id_type=MESH,
            )

        for off in range(1, n):
            share(off, False).start()
        for off in range(1, n):
            share(off, True).wait_recv()
        total = red[start]
        for j in range(1, n):
            total = total + red[start + j]
        for off in range(1, n):
            share(off, False).wait_send()
        start += n
    cells = 3.0 * nx * ny * nz * sizes[0] * sizes[1] * sizes[2]
    root = jnp.sqrt(jnp.sum(total, axis=1, keepdims=True) / cells + tiny_mean)
    spread = jnp.where(lane == sub % 4, root, 0.0)
    upper = jnp.sum(jnp.where(sub < 4, spread, 0.0), axis=0, keepdims=True)
    lower = jnp.sum(jnp.where(sub < 4, 0.0, spread), axis=0, keepdims=True)
    norms_ref[...] = jnp.concatenate([upper, lower], axis=0)[:, :4]

    for o in offs:
        @pl.when(exists(o))
        def _():
            copy_of(o).wait_send()


def body(velocity, direction, pressure, body_force, phase_ids, creep, exponent, yields, accepted):
    sizes = tuple(lax.axis_size(a) for a in AXES)
    tile = velocity.shape[2:]
    vmem = pl.BlockSpec(memory_space=pltpu.VMEM)
    smem = pl.BlockSpec(memory_space=pltpu.SMEM)
    slots = sum(sizes)

    def scratch(*lead):
        return pltpu.VMEM(lead + tile, jnp.float32)

    return pl.pallas_call(
        functools.partial(kernel, sizes),
        out_shape=(
            jax.ShapeDtypeStruct((2, 4), jnp.float32),
            jax.ShapeDtypeStruct(velocity.shape, jnp.float32),
            jax.ShapeDtypeStruct(velocity.shape, jnp.float32),
        ),
        in_specs=[smem] * 4 + [vmem] * 5,
        out_specs=(vmem, vmem, vmem),
        scratch_shapes=[
            scratch(2, 14), scratch(2, 14), scratch(2, 2), scratch(2, 3),
            scratch(2, 14), scratch(2, 14), scratch(2, 2), scratch(2, 2),
            scratch(2, 2, 2), scratch(2, 2, 3),
            scratch(36, velocity.shape[1]), scratch(2, 18), scratch(2, 18), scratch(slots),
            pltpu.SemaphoreType.DMA((18,)), pltpu.SemaphoreType.DMA((18,)),
            pltpu.SemaphoreType.DMA((slots,)), pltpu.SemaphoreType.DMA((slots,)),
        ],
        compiler_params=pltpu.CompilerParams(collective_id=0, has_side_effects=True),
    )(creep, exponent, yields, accepted, velocity, direction, pressure, body_force, phase_ids)


def solution(mesh):
    placed = (
        P(None, "gx", "gy", "gz"),
        P(None, "gx", "gy", "gz"),
        P("gx", "gy", "gz"),
        P(None, "gx", "gy", "gz"),
        P("gx", "gy", "gz"),
        P(),
        P(),
        P(),
        P(),
    )
    return jax.shard_map(
        body,
        mesh=mesh,
        in_specs=placed,
        out_specs=(P(), P(None, "gx", "gy", "gz"), P(None, "gx", "gy", "gz")),
        check_vma=False,
    )
```

time: 139 us -> 37.8 us (0.27)
  starting transfers between devices: 48.1 us -> 0 us
  blocking collectives: 40.2 us -> 0 us
  Pallas kernels: 0 us -> 32.9 us
  other arithmetic: 20.8 us -> 0 us
  waiting for transfers between devices: 12.4 us -> 0 us
  local copies, waits for them, and re-layouts: 15 us -> 3.41 us
    ppermute x18 -> x0, starting transfers between devices: 48.1 us -> none  [the longest x9 36.3 us: extended(): before = lax.ppermute(last, axis, up)]
    psum x1 -> x0, blocking collectives: 40.2 us -> none  [body(): sums = lax.psum(jnp.stack(actual + predicted), ('gx', 'gy', 'gz'))]
    pallas_call x0 -> x1, Pallas kernels: none -> 32.9 us  [body(): pl.pallas_call(functools.partial(kernel, sizes), out_shape=(jax.ShapeDtyp...]
    ppermute x18 -> x0, waiting for transfers between devices: 12.4 us -> none  [the longest x9 11.9 us: extended(): after = lax.ppermute(leading, axis, down)]
    mul x8 -> x0, other arithmetic: 8.76 us -> none  [the longest x2 3.93 us: stress_stack(): trial_stress = 2.0 * spread_cells(trial_viscosity) * trial_rates]
    another operation x5 -> x0, local copies, waits for them, and re-layouts: 5.38 us -> none  [the longest x1 5.04 us: body(): sums = lax.psum(jnp.stack(actual + predicted), ('gx', 'gy', 'gz'))]
    another operation x7 -> x0, other arithmetic: 4.53 us -> none  [the longest x1 1.81 us: body(): jnp.stack([paired[0] + length * paired[1] for length in step_lengths])]
    reduce_sum x3 -> x0, other arithmetic: 2.94 us -> none  [the longest x1 1.33 us: body(): actual.append(jnp.sum(trial_residual * trial_residual))]
  transfers between devices with their start and end apart: 18 -> 0, of which waited for: 5 -> 0; matrix products, arithmetic and copies ran while one was open for 4% -> 0% of each run, Pallas kernels for 0% -> 0%
where the time goes in v1:
time: 37.8 us; the launch traced here: 37.6 us
  Pallas kernels  32.9 us (87%)
  local copies, waits for them, and re-layouts  3.41 us (9%)
  between operations  1.3 us (3%)
    pallas_call x1, Pallas kernels, body(): pl.pallas_call(functools.partial(kernel, sizes), out_shape=(jax.ShapeDtyp...  32.9 us
    unnamed x7, local copies, waits for them, and re-layouts  3.41 us

profile of v1, /device:TPU:0, one launch (start us, length us, event | category | flops | bytes accessed | tf_op | source)
XLA Modules:
  0.0 37.6 jit_solution(18149692107539297886)
XLA Ops:
  1.3 32.9 %shard_map.112 = (f32[2,4]{1,0:T(2,128)}, f32[3,8,8,128]{3,2,1,0:T(8,128)}, f32[3,8,8,128]{3,2,1,0:T(8,128)}) custom-call(f32[4]{0:T(128)} %creep_ref.1, f32[4]{0:T(128)} %exponent_ref.1, f32[4]{0:T(128)} %yield_ref.1, s32[1]{0:T(128)S(6)} %copy.15.accepted_ref, f32[3,8,8,128]{3,2,1,0:T(8,128)} %v_ref.1, f32[3,8,8,128]{3,2,1,0:T(8,128)} %d_ref.1, ...), custom_call_target="tpu_custom_call" | custom-call | tf_op jit(solution)/shard_map/pallas_call | solution.py:410
  34.2 0.0 copy-start.1
  34.2 0.6 %copy-done.1 = f32[2,4]{1,0:T(2,128)S(1)} copy-done((f32[2,4]{1,0:T(2,128)S(1)}, f32[2,4]{1,0:T(2,128)}, u32[]{:S(2)}) %copy-start.1) | copy-done | bytes 56
  34.8 0.6 %copy.16 = f32[2,4]{1,0:T(2,128)} copy(f32[2,4]{1,0:T(2,128)S(1)} %copy-done.1) | data formatting | bytes 64
  35.4 0.0 copy-start
  35.4 1.6 %copy.17 = f32[3,8,8,128]{3,2,1,0:T(8,128)} copy(f32[3,8,8,128]{3,2,1,0:T(8,128)} %get-tuple-element.7) | data formatting | bytes 196608
  36.9 0.0 copy-done
  36.9 0.6 %copy.18 = f32[3,8,8,128]{3,2,1,0:T(8,128)} copy(f32[3,8,8,128]{3,2,1,0:T(8,128)S(1)} %copy-done) | data formatting | bytes 196608
Async XLA Ops:
  34.2 0.6 %copy-start.1 = (f32[2,4]{1,0:T(2,128)S(1)}, f32[2,4]{1,0:T(2,128)}, u32[]{:S(2)}) copy-start(f32[2,4]{1,0:T(2,128)} %get-tuple-element.6) | copy-start | bytes 100
  35.4 1.6 %copy-start = (f32[3,8,8,128]{3,2,1,0:T(8,128)S(1)}, f32[3,8,8,128]{3,2,1,0:T(8,128)}, u32[]{:S(2)}) copy-start(f32[3,8,8,128]{3,2,1,0:T(8,128)} %get-tuple-element.8) | copy-start | bytes 294916

commit v2 on v1

v2 whole, which is shorter than its diff:
```python
import functools

import jax
import jax.numpy as jnp
from jax import lax
from jax.experimental import pallas as pl
from jax.experimental.pallas import tpu as pltpu
from jax.sharding import PartitionSpec as P

step_lengths = (1.0, 0.5, 0.25, 0.125)
rate_offset = 0.01
viscosity_least = 0.05
tiny_mean = 1e-06
MESH = pl.DeviceIdType.MESH
AXES = ("gx", "gy", "gz")
INV_LN2 = 1.4426950408889634
FACE_COMPONENTS = ((0, 3, 4), (3, 1, 5), (4, 5, 2))


def spin(values, shift, axis):
    return pltpu.roll(values, shift % values.shape[axis], axis)


def offsets():
    found = []
    for dx in (-1, 0, 1):
        for dy in (-1, 0, 1):
            for dz in (-1, 0, 1):
                if 1 <= abs(dx) + abs(dy) + abs(dz) <= 2:
                    found.append((dx, dy, dz))
    return sorted(found, key=lambda o: (o[2] != 0, sum(map(abs, o))))


def stress_fields(E, F, phase, params, components, mask):
    factors, powers, yields = params
    factor, power, half_yield = factors[-1], powers[-1], yields[-1]
    for k in range(len(factors) - 2, -1, -1):
        here = phase == float(k)
        factor = jnp.where(here, factors[k], factor)
        power = jnp.where(here, powers[k], power)
        half_yield = jnp.where(here, yields[k], half_yield)

    def dot(a, b):
        diagonal = a[0] * b[0] + a[1] * b[1] + a[2] * b[2]
        return diagonal + 2.0 * (a[3] * b[3] + a[4] * b[4] + a[5] * b[5])

    def parts(rates):
        second = 0.125 * dot(rates, rates) + rate_offset
        creep = factor * jnp.exp2(power * jnp.log(second))
        plastic = half_yield * lax.rsqrt(second)
        total = creep + plastic
        inverse = 1.0 / total
        return second, creep, plastic, inverse, creep * plastic * inverse

    second, creep, plastic, inverse, mixed = parts(E)
    half = 0.5 * mixed + 0.5 * viscosity_least
    slope = mixed * (plastic * (power * (1.0 / INV_LN2)) - 0.5 * creep) * inverse / second
    coupling = 0.125 * slope * dot(E, F)
    if mask is not None:
        half = half * mask
        coupling = coupling * mask
    fields = [[half * E[i] for i in components]]
    fields.append([half * F[i] + coupling * E[i] for i in components])
    for length in step_lengths:
        rates = [e + length * f if length != 1.0 else e + f for e, f in zip(E, F)]
        half = 0.5 * parts(rates)[4] + 0.5 * viscosity_least
        if mask is not None:
            half = half * mask
        fields.append([half * rates[i] for i in components])
    return fields


def twice_rates(g):
    return [
        g[0][0],
        g[1][1],
        g[2][2],
        0.5 * (g[0][1] + g[1][0]),
        0.5 * (g[0][2] + g[2][0]),
        0.5 * (g[1][2] + g[2][1]),
    ]


def kernel(
    sizes,
    creep_ref, exponent_ref, yield_ref, accepted_ref,
    v_hbm, d_hbm, p_hbm, b_hbm, m_hbm,
    norms_ref, cv_ref, cr_ref,
    vx, px, mx, bx, sy, sxy, sz, ry, yr, rz, rxz, ryz,
    w3, grads, stress, phases, masks, red,
    load_sem, send_sem, recv_sem, red_send, red_recv,
):
    nx, ny, nz = v_hbm.shape[1:]
    me = [lax.axis_index(a) for a in AXES]
    devices = sizes[0] * sizes[1] * sizes[2]
    rank = (me[0] * sizes[1] + me[1]) * sizes[2] + me[2]
    offs = offsets()

    loads = [
        pltpu.make_async_copy(source, target, load_sem.at[n])
        for n, (source, target) in enumerate((
            (v_hbm, vx.at[pl.ds(0, 3), pl.ds(2, nx)]),
            (d_hbm, vx.at[pl.ds(3, 3), pl.ds(2, nx)]),
            (p_hbm, px.at[pl.ds(1, nx)]),
            (m_hbm, mx.at[pl.ds(1, nx)]),
            (b_hbm, bx),
        ))
    ]
    for load in loads:
        load.start()

    def mate(k):
        other = lax.rem(rank + k, devices)
        return (
            other // (sizes[1] * sizes[2]),
            lax.rem(other // sizes[2], sizes[1]),
            lax.rem(other, sizes[2]),
        )

    barrier = pltpu.get_barrier_semaphore()

    def greet(k, carry):
        pl.semaphore_signal(barrier, inc=1, device_id=mate(k), device_id_type=MESH)
        return carry

    lax.fori_loop(1, devices, greet, 0)

    inner = [(me[k] > 0, me[k] < sizes[k] - 1) for k in range(3)]

    def exists(o):
        ok = None
        for k in range(3):
            if o[k]:
                here = inner[k][(o[k] + 1) // 2]
                ok = here if ok is None else jnp.logical_and(ok, here)
        return ok

    def device(o):
        return tuple(me[k] + o[k] for k in range(3))

    sub = lax.broadcasted_iota(jnp.int32, (ny, nz), 0)
    lane = lax.broadcasted_iota(jnp.int32, (ny, nz), 1)
    quad = lane % 4
    first, last = lane == 0, lane == nz - 1
    top, bottom = sub == 0, sub == ny - 1
    is_left = quad < 2

    for load in loads[:4]:
        load.wait()

    def gather(x, packs):
        packs = list(packs)
        for e in range(8):
            if e < 6:
                plane = vx[e, x + 2]
            else:
                plane = px[x + 1] if e == 6 else mx[x + 1].astype(jnp.float32)
            base = 4 * ((e % 4) * nx + x)
            turned = pltpu.roll(plane, lax.rem(base + 2, nz), 1)
            packs[e // 4] = jnp.where(lane // 4 == base // 4, turned, packs[e // 4])
        for s in range(2):
            near, far = (0, 1) if s == 0 else (ny - 1, ny - 2)
            for c in range(6):
                sy[s, 2 * c, pl.ds(x, 1), :] = vx[c, x + 2, pl.ds(near, 1), :]
                sy[s, 2 * c + 1, pl.ds(x, 1), :] = vx[c, x + 2, pl.ds(far, 1), :]
            sy[s, 12, pl.ds(x, 1), :] = px[x + 1, pl.ds(near, 1), :]
            sy[s, 13, pl.ds(x, 1), :] = mx[x + 1, pl.ds(near, 1), :].astype(jnp.float32)
        return tuple(packs)

    blank = jnp.zeros((ny, nz), jnp.float32)
    packs = lax.fori_loop(0, nx, gather, (blank, blank))
    for s in range(2):
        near = 0 if s == 0 else ny - 1
        edge = blank
        for c in range(6):
            edge = jnp.where(lane // 2 == c, spin(sy[s, 2 * c], 2 * c + 1, 1), edge)
            for side in range(2):
                sxy[side, s, c] = vx[c, 2 + side * (nx - 1), pl.ds(near, 1), :]
        sz[s, 0] = packs[0]
        sz[s, 1] = packs[1]
        sz[s, 2] = edge

    def ends(o):
        side = [(k + 1) // 2 for k in o]
        back = [1 - k for k in side]
        dx, dy, dz = o
        if dx and dy:
            return [(sxy.at[side[0], side[1]], yr.at[back[1], back[0] * (nx + 1), pl.ds(0, 6)])]
        if dx and dz:
            return [(sz.at[0, pl.ds(0, 2)], rxz.at[back[0], back[2]])]
        if dy and dz:
            return [(sz.at[side[1]], ryz.at[back[1], back[2]])]
        if dx:
            mine, theirs = (2, nx + 2) if dx < 0 else (nx, 0)
            one, other = (1, nx + 1) if dx < 0 else (nx, 0)
            return [
                (vx.at[:, pl.ds(mine, 2)], vx.at[:, pl.ds(theirs, 2)]),
                (px.at[one], px.at[other]),
                (mx.at[one], mx.at[other]),
            ]
        if dy:
            return [(sy.at[side[1]], ry.at[back[1]])]
        return [(sz.at[0, pl.ds(0, 2)], rz.at[back[2]])]

    def copies_of(o):
        mirror = tuple(-k for k in o)
        return [
            pltpu.make_async_remote_copy(
                src_ref=source, dst_ref=target,
                send_sem=send_sem.at[offs.index(o), n], recv_sem=recv_sem.at[offs.index(mirror), n],
                device_id=device(o), device_id_type=MESH,
            )
            for n, (source, target) in enumerate(ends(o))
        ]

    pl.semaphore_wait(barrier, devices - 1)
    for o in offs:
        @pl.when(exists(o))
        def _():
            for copy in copies_of(o):
                copy.start()

    accepted = accepted_ref[0]
    length = jnp.float32(step_lengths[-1])
    for k in range(len(step_lengths) - 2, -1, -1):
        length = jnp.where(accepted == k, jnp.float32(step_lengths[k]), length)

    def ahead(x, carry):
        for c in range(3):
            cv_ref[c, x] = vx[c, x + 2] + length * vx[c + 3, x + 2]
        phases[x + 1] = mx[x + 1].astype(jnp.float32)
        masks[x + 1] = jnp.ones((ny, nz), jnp.float32)
        return carry

    lax.fori_loop(0, nx, ahead, 0)

    full = lambda value: jnp.full((ny, nz), value, jnp.float32)
    count = creep_ref.shape[0]
    factors = [full(creep_ref[k]) for k in range(count)]
    halves = [0.5 * full(yield_ref[k]) for k in range(count)]
    powers = []
    for k in range(count):
        n = full(exponent_ref[k])
        powers.append((1.0 - n) / (2.0 * n) * INV_LN2)
    params = (factors, powers, halves)

    def scale_of(o):
        return jnp.full((ny, nz), exists(o).astype(jnp.float32))

    for s in range(2):
        masks[s * (nx + 1)] = scale_of((2 * s - 1, 0, 0))
        masks[nx + 2 + s] = scale_of((0, 2 * s - 1, 0))
    masks[nx + 4] = jnp.where(
        quad == 1, scale_of((0, 0, -1)), jnp.where(quad == 2, scale_of((0, 0, 1)), 0.0)
    )

    for o in offs:
        mirror = tuple(-k for k in o)

        @pl.when(exists(o))
        def _():
            for copy in copies_of(mirror):
                copy.wait_recv()

        @pl.when(jnp.logical_not(exists(o)))
        def _():
            for _, target in ends(mirror):
                target[...] = jnp.zeros(target.shape, target.dtype)

    def along_y(V, before, after):
        down = spin(jnp.where(bottom, before, V), 1, 0)
        up = spin(jnp.where(top, after, V), -1, 0)
        return up - down

    def along_z(V, T):
        down = spin(jnp.where(last, T, V), 1, 1)
        up = spin(jnp.where(first, T, V), -1, 1)
        return up - down

    for h in range(2):
        w3[1, h] = jnp.where(is_left, rz[0, h], rz[1, h])
        for s in range(2):
            w3[2 * s, h] = jnp.where(is_left, rxz[s, 0, h], rxz[s, 1, h])

    def rows(x, carry):
        for s in range(2):
            for c in range(7):
                yr[s, x + 1, c] = ry[s, 2 * c, pl.ds(x, 1), :]
        return carry

    lax.fori_loop(0, nx, rows, 0)
    for s in range(2):
        phases[s * (nx + 1)] = mx[s * (nx + 1)].astype(jnp.float32)
        phases[nx + 2 + s] = ry[s, 13]

    def inside(q, carry):
        third = jnp.where(q == 0, 0, jnp.where(q == nx + 1, 2, 1))
        x = lax.rem(q + nx - 1, nx)
        for c in range(6):
            V = vx[c, q + 1]
            T = pltpu.roll(w3[third, c // 4], nz - (4 * ((c % 4) * nx + x) + 2), 1)
            grads[3 * c, q] = vx[c, q + 2] - vx[c, q]
            grads[3 * c + 1, q] = along_y(V, yr[0, q, c], yr[1, q, c])
            grads[3 * c + 2, q] = along_z(V, T)
        return carry

    lax.fori_loop(0, nx + 2, inside, 0)

    def sides(s, carry):
        sign = jnp.where(s == 0, jnp.float32(1.0), jnp.float32(-1.0))
        E = jnp.where(lane % 2 == 0, ryz[s, 0, 2], ryz[s, 1, 2])
        for c in range(6):
            B = ry[s, 2 * c]
            grads[3 * c, nx + 2 + s] = along_y(B, yr[s, 0, c], yr[s, nx + 1, c])
            grads[3 * c + 1, nx + 2 + s] = sign * (sy[s, 2 * c] - ry[s, 2 * c + 1])
            grads[3 * c + 2, nx + 2 + s] = along_z(B, spin(E, -(2 * c + 1), 1))
        return carry

    lax.fori_loop(0, 2, sides, 0)

    spot = (lane // 4) % nx
    turn = 4 * (nx - 1)
    for h in range(2):
        O, W = sz[0, h], w3[1, h]
        dz = jnp.where(quad == 1, spin(O, -1, 1) - spin(W, 1, 1), spin(W, -1, 1) - spin(O, 1, 1))
        down = jnp.where(spot == 0, spin(w3[0, h], -turn, 1), spin(W, 4, 1))
        up = jnp.where(spot == nx - 1, spin(w3[2, h], turn, 1), spin(W, -4, 1))
        before = jnp.where(is_left, ryz[0, 0, h], ryz[0, 1, h])
        after = jnp.where(is_left, ryz[1, 0, h], ryz[1, 1, h])
        packed = (up - down, along_y(W, before, after), dz)
        for c in range(4 * h, min(4 * h + 4, 6)):
            for j in range(3):
                grads[3 * c + j, nx + 4] = spin(packed[j], -4 * nx * (c % 4), 1)
    phases[nx + 4] = spin(w3[1, 1], -4 * nx * 3, 1)

    def stresses(q, carry):
        g = [[grads[3 * c + j, q] for j in range(3)] for c in range(6)]
        fields = stress_fields(
            twice_rates(g[:3]), twice_rates(g[3:]), phases[q], params, range(6), masks[q]
        )
        for f in range(6):
            for i in range(6):
                stress[6 * f + i, q] = fields[f][i]
        return carry

    lax.fori_loop(0, nx + 5, stresses, 0)
    loads[4].wait()

    def residuals(x, sums):
        sums = list(sums)
        turn = nz - (4 * x + 2)
        T = pltpu.roll(w3[1, 1], nz - (4 * (2 * nx + x) + 2), 1)
        slopes = (
            px[x + 2] - px[x],
            along_y(px[x + 1], yr[0, x + 1, 6], yr[1, x + 1, 6]),
            along_z(px[x + 1], T),
        )
        for i in range(3):
            a, b, c = (FACE_COMPONENTS[j][i] for j in range(3))
            loading = bx[i, x] - 0.5 * slopes[i]
            divided = []
            for f in range(6):
                dx = stress[6 * f + a, x + 2] - stress[6 * f + a, x]
                dy = along_y(
                    stress[6 * f + b, x + 1],
                    stress[6 * f + b, nx + 2, pl.ds(x, 1), :],
                    stress[6 * f + b, nx + 3, pl.ds(x, 1), :],
                )
                dz = along_z(stress[6 * f + c, x + 1], pltpu.roll(stress[6 * f + c, nx + 4], turn, 1))
                divided.append(dx + dy + dz)
            base = divided[0] + loading
            chosen = None
            for k in range(3, -1, -1):
                residual = divided[2 + k] + loading
                linear = base + step_lengths[k] * divided[1]
                sums[k] = sums[k] + residual * residual
                sums[4 + k] = sums[4 + k] + linear * linear
                chosen = residual if chosen is None else jnp.where(accepted == k, residual, chosen)
            cr_ref[i, x] = chosen
        return tuple(sums)

    sums = lax.fori_loop(0, nx, residuals, (blank,) * 8)

    total = blank
    for k in range(8):
        total = jnp.where(sub == k, jnp.sum(sums[k], axis=0, keepdims=True), total)
    total = jnp.sum(total, axis=1, keepdims=True)
    red[rank] = jnp.sum(jnp.where(lane == sub, total, 0.0), axis=0, keepdims=True)

    def share(k, carry):
        pltpu.make_async_remote_copy(
            src_ref=red.at[rank], dst_ref=red.at[rank], send_sem=red_send, recv_sem=red_recv,
            device_id=mate(k), device_id_type=MESH,
        ).start()
        return carry

    lax.fori_loop(1, devices, share, 0)
    others = red.at[pl.ds(0, devices - 1)]
    pltpu.make_async_copy(others, others, red_recv).wait()
    total = jnp.sum(red[...], axis=0)
    cells = 3.0 * nx * ny * nz * devices
    root = jnp.sqrt(total / cells + tiny_mean)
    norms_ref[0:1, :] = root[:, :4]
    norms_ref[1:2, :] = spin(jnp.broadcast_to(root, (ny, nz)), -4, 1)[0:1, :4]

    pltpu.make_async_copy(others, others, red_send).wait()
    for o in offs:
        @pl.when(exists(o))
        def _():
            for copy in copies_of(o):
                copy.wait_send()


def body(velocity, direction, pressure, body_force, phase_ids, creep, exponent, yields, accepted):
    sizes = tuple(lax.axis_size(a) for a in AXES)
    nx = velocity.shape[1]
    tile = velocity.shape[2:]
    row = (1, tile[1])
    vmem = pl.BlockSpec(memory_space=pltpu.VMEM)
    smem = pl.BlockSpec(memory_space=pltpu.SMEM)
    hbm = pl.BlockSpec(memory_space=pl.ANY)

    def scratch(*lead, held=jnp.float32, shape=tile):
        return pltpu.VMEM(lead + shape, held)

    return pl.pallas_call(
        functools.partial(kernel, sizes),
        out_shape=(
            jax.ShapeDtypeStruct((2, 4), jnp.float32),
            jax.ShapeDtypeStruct(velocity.shape, jnp.float32),
            jax.ShapeDtypeStruct(velocity.shape, jnp.float32),
        ),
        in_specs=[smem] * 4 + [hbm] * 5,
        out_specs=(vmem, vmem, vmem),
        scratch_shapes=[
            scratch(6, nx + 4), scratch(nx + 2), scratch(nx + 2, held=jnp.int32), scratch(3, nx),
            scratch(2, 14), scratch(2, 2, 6, shape=row), scratch(2, 3),
            scratch(2, 14), scratch(2, nx + 2, 7, shape=row), scratch(2, 2),
            scratch(2, 2, 2), scratch(2, 2, 3),
            scratch(3, 2), scratch(18, nx + 5), scratch(36, nx + 5), scratch(nx + 5), scratch(nx + 5),
            scratch(sizes[0] * sizes[1] * sizes[2], shape=row),
            pltpu.SemaphoreType.DMA((5,)),
            pltpu.SemaphoreType.DMA((18, 3)), pltpu.SemaphoreType.DMA((18, 3)),
            pltpu.SemaphoreType.DMA, pltpu.SemaphoreType.DMA,
        ],
        compiler_params=pltpu.CompilerParams(collective_id=0, has_side_effects=True),
    )(creep, exponent, yields, accepted, velocity, direction, pressure, body_force, phase_ids)


def solution(mesh):
    placed = (
        P(None, "gx", "gy", "gz"),
        P(None, "gx", "gy", "gz"),
        P("gx", "gy", "gz"),
        P(None, "gx", "gy", "gz"),
        P("gx", "gy", "gz"),
        P(),
        P(),
        P(),
        P(),
    )
    return jax.shard_map(
        body,
        mesh=mesh,
        in_specs=placed,
        out_specs=(P(), P(None, "gx", "gy", "gz"), P(None, "gx", "gy", "gz")),
        check_vma=False,
    )
```

time: 37.8 us -> 26.3 us (0.70)
  Pallas kernels: 32.9 us -> 21.3 us
    pallas_call x1, Pallas kernels: 32.9 us -> 21.3 us  [body(): pl.pallas_call(functools.partial(kernel, sizes), out_shape=(jax.ShapeDtyp...]
where the time goes in v2:
time: 26.3 us; the launch traced here: 26.1 us
  Pallas kernels  21.3 us (81%)
  local copies, waits for them, and re-layouts  3.41 us (13%)
  between operations  1.3 us (5%)
    pallas_call x1, Pallas kernels, body(): pl.pallas_call(functools.partial(kernel, sizes), out_shape=(jax.ShapeDtyp...  21.3 us
    unnamed x7, local copies, waits for them, and re-layouts  3.41 us

profile of v2, /device:TPU:0, one launch (start us, length us, event | category | flops | bytes accessed | tf_op | source)
XLA Modules:
  0.0 26.1 jit_solution(1499378376883411993)
XLA Ops:
  1.3 21.3 %shard_map.112 = (f32[2,4]{1,0:T(2,128)}, f32[3,8,8,128]{3,2,1,0:T(8,128)}, f32[3,8,8,128]{3,2,1,0:T(8,128)}) custom-call(f32[4]{0:T(128)} %creep_ref.1, f32[4]{0:T(128)} %exponent_ref.1, f32[4]{0:T(128)} %yield_ref.1, s32[1]{0:T(128)S(6)} %copy.15.accepted_ref, f32[3,8,8,128]{3,2,1,0:T(8,128)} %v_hbm.1, f32[3,8,8,128]{3,2,1,0:T(8,128)} %d_hbm.1, ...), custom_call_target="tpu_custom_call" | custom-call | tf_op jit(solution)/shard_map/pallas_call | solution.py:426
  22.6 0.0 copy-start.1
  22.6 0.6 %copy-done.1 = f32[2,4]{1,0:T(2,128)S(1)} copy-done((f32[2,4]{1,0:T(2,128)S(1)}, f32[2,4]{1,0:T(2,128)}, u32[]{:S(2)}) %copy-start.1) | copy-done | bytes 56
  23.3 0.6 %copy.16 = f32[2,4]{1,0:T(2,128)} copy(f32[2,4]{1,0:T(2,128)S(1)} %copy-done.1) | data formatting | bytes 64
  23.8 0.0 copy-start
  23.8 1.6 %copy.17 = f32[3,8,8,128]{3,2,1,0:T(8,128)} copy(f32[3,8,8,128]{3,2,1,0:T(8,128)} %get-tuple-element.7) | data formatting | bytes 196608
  25.4 0.0 copy-done
  25.4 0.6 %copy.18 = f32[3,8,8,128]{3,2,1,0:T(8,128)} copy(f32[3,8,8,128]{3,2,1,0:T(8,128)S(1)} %copy-done) | data formatting | bytes 196608
Async XLA Ops:
  22.6 0.6 %copy-start.1 = (f32[2,4]{1,0:T(2,128)S(1)}, f32[2,4]{1,0:T(2,128)}, u32[]{:S(2)}) copy-start(f32[2,4]{1,0:T(2,128)} %get-tuple-element.6) | copy-start | bytes 100
  23.8 1.6 %copy-start = (f32[3,8,8,128]{3,2,1,0:T(8,128)S(1)}, f32[3,8,8,128]{3,2,1,0:T(8,128)}, u32[]{:S(2)}) copy-start(f32[3,8,8,128]{3,2,1,0:T(8,128)} %get-tuple-element.8) | copy-start | bytes 294916

commit v3 on v2

--- a/solution.py
+++ b/solution.py
@@ -28,7 +28,7 @@
             for dz in (-1, 0, 1):
                 if 1 <= abs(dx) + abs(dy) + abs(dz) <= 2:
                     found.append((dx, dy, dz))
-    return sorted(found, key=lambda o: (o[2] != 0, sum(map(abs, o))))
+    return sorted(found, key=lambda o: (-sum(map(abs, o)), o[2] == 0))
 
 
 def stress_fields(E, F, phase, params, components, mask):
@@ -85,10 +85,10 @@
     sizes,
     creep_ref, exponent_ref, yield_ref, accepted_ref,
     v_hbm, d_hbm, p_hbm, b_hbm, m_hbm,
-    norms_ref, cv_ref, cr_ref,
-    vx, px, mx, bx, sy, sxy, sz, ry, yr, rz, rxz, ryz,
+    norms_ref, cr_hbm,
+    cr_ref, vx, px, mx, bx, sy, sxy, sz, ry, yr, rz, rxz, ryz,
     w3, grads, stress, phases, masks, red,
-    load_sem, send_sem, recv_sem, red_send, red_recv,
+    load_sem, out_sem, send_sem, recv_sem, red_send, red_recv,
 ):
     nx, ny, nz = v_hbm.shape[1:]
     me = [lax.axis_index(a) for a in AXES]
@@ -221,18 +221,14 @@
                 copy.start()
 
     accepted = accepted_ref[0]
-    length = jnp.float32(step_lengths[-1])
-    for k in range(len(step_lengths) - 2, -1, -1):
-        length = jnp.where(accepted == k, jnp.float32(step_lengths[k]), length)
 
     def ahead(x, carry):
-        for c in range(3):
-            cv_ref[c, x] = vx[c, x + 2] + length * vx[c + 3, x + 2]
         phases[x + 1] = mx[x + 1].astype(jnp.float32)
         masks[x + 1] = jnp.ones((ny, nz), jnp.float32)
         return carry
 
     lax.fori_loop(0, nx, ahead, 0)
+    cr_out = pltpu.make_async_copy(cr_ref, cr_hbm, out_sem)
 
     full = lambda value: jnp.full((ny, nz), value, jnp.float32)
     count = creep_ref.shape[0]
@@ -396,6 +392,7 @@
 
     lax.fori_loop(1, devices, share, 0)
     others = red.at[pl.ds(0, devices - 1)]
+    cr_out.start()
     pltpu.make_async_copy(others, others, red_recv).wait()
     total = jnp.sum(red[...], axis=0)
     cells = 3.0 * nx * ny * nz * devices
@@ -404,11 +401,22 @@
     norms_ref[1:2, :] = spin(jnp.broadcast_to(root, (ny, nz)), -4, 1)[0:1, :4]
 
     pltpu.make_async_copy(others, others, red_send).wait()
+    cr_out.wait()
     for o in offs:
         @pl.when(exists(o))
         def _():
             for copy in copies_of(o):
                 copy.wait_send()
+
+
+def finish(accepted_ref, n_ref, v_ref, d_ref, r_ref, norms_ref, cv_ref, cr_ref):
+    accepted = accepted_ref[0]
+    length = jnp.float32(step_lengths[-1])
+    for k in range(len(step_lengths) - 2, -1, -1):
+        length = jnp.where(accepted == k, jnp.float32(step_lengths[k]), length)
+    cv_ref[...] = v_ref[...] + length * d_ref[...]
+    cr_ref[...] = r_ref[...]
+    norms_ref[...] = n_ref[...]
 
 
 def body(velocity, direction, pressure, body_force, phase_ids, creep, exponent, yields, accepted):
@@ -423,28 +431,38 @@
     def scratch(*lead, held=jnp.float32, shape=tile):
         return pltpu.VMEM(lead + shape, held)
 
-    return pl.pallas_call(
+    norms, residual = pl.pallas_call(
         functools.partial(kernel, sizes),
         out_shape=(
             jax.ShapeDtypeStruct((2, 4), jnp.float32),
             jax.ShapeDtypeStruct(velocity.shape, jnp.float32),
-            jax.ShapeDtypeStruct(velocity.shape, jnp.float32),
         ),
         in_specs=[smem] * 4 + [hbm] * 5,
-        out_specs=(vmem, vmem, vmem),
+        out_specs=(vmem, hbm),
         scratch_shapes=[
+            scratch(3, nx),
             scratch(6, nx + 4), scratch(nx + 2), scratch(nx + 2, held=jnp.int32), scratch(3, nx),
             scratch(2, 14), scratch(2, 2, 6, shape=row), scratch(2, 3),
             scratch(2, 14), scratch(2, nx + 2, 7, shape=row), scratch(2, 2),
             scratch(2, 2, 2), scratch(2, 2, 3),
             scratch(3, 2), scratch(18, nx + 5), scratch(36, nx + 5), scratch(nx + 5), scratch(nx + 5),
             scratch(sizes[0] * sizes[1] * sizes[2], shape=row),
-            pltpu.SemaphoreType.DMA((5,)),
+            pltpu.SemaphoreType.DMA((5,)), pltpu.SemaphoreType.DMA,
             pltpu.SemaphoreType.DMA((18, 3)), pltpu.SemaphoreType.DMA((18, 3)),
             pltpu.SemaphoreType.DMA, pltpu.SemaphoreType.DMA,
         ],
         compiler_params=pltpu.CompilerParams(collective_id=0, has_side_effects=True),
     )(creep, exponent, yields, accepted, velocity, direction, pressure, body_force, phase_ids)
+    return pl.pallas_call(
+        finish,
+        out_shape=(
+            jax.ShapeDtypeStruct((2, 4), jnp.float32),
+            jax.ShapeDtypeStruct(velocity.shape, jnp.float32),
+            jax.ShapeDtypeStruct(velocity.shape, jnp.float32),
+        ),
+        in_specs=[smem] + [vmem] * 4,
+        out_specs=(vmem, vmem, vmem),
+    )(accepted, norms, velocity, direction, residual)
 
 
 def solution(mesh):

time: 26.3 us -> 24 us (0.913)
  local copies, waits for them, and re-layouts: 3.41 us -> 0 us
  Pallas kernels: 21.3 us -> 22.5 us
    unnamed x7 -> x0, local copies, waits for them, and re-layouts: 3.41 us -> none
    pallas_call x0 -> x1, Pallas kernels: none -> 1.68 us  [body(): pl.pallas_call(finish, out_shape=(jax.ShapeDtypeStruct((2, 4), jnp.float3...]
    pallas_call x1, Pallas kernels: 21.3 us -> 20.8 us  [body(): pl.pallas_call(functools.partial(kernel, sizes), out_shape=(jax.ShapeDtyp...]
where the time goes in v3:
time: 24 us; the launch traced here: 23.8 us
  Pallas kernels  22.5 us (94%)
  between operations  1.29 us (5%)
    pallas_call x1, Pallas kernels, body(): pl.pallas_call(functools.partial(kernel, sizes), out_shape=(jax.ShapeDtyp...  20.8 us
    pallas_call x1, Pallas kernels, body(): pl.pallas_call(finish, out_shape=(jax.ShapeDtypeStruct((2, 4), jnp.float3...  1.68 us

profile of v3, /device:TPU:0, one launch (start us, length us, event | category | flops | bytes accessed | tf_op | source)
XLA Modules:
  0.0 23.8 jit_solution(8786977567267870286)
XLA Ops:
  1.3 20.8 %shard_map.112 = (f32[2,4]{1,0:T(2,128)}, f32[3,8,8,128]{3,2,1,0:T(8,128)}) custom-call(f32[4]{0:T(128)} %creep_ref.1, f32[4]{0:T(128)} %exponent_ref.1, f32[4]{0:T(128)} %yield_ref.1, s32[1]{0:T(128)S(6)} %copy.12.accepted_ref, f32[3,8,8,128]{3,2,1,0:T(8,128)} %v_ref.1, f32[3,8,8,128]{3,2,1,0:T(8,128)} %d_ref.1, f32[8,8,128]{2,1,0:T(8,128)} %p_hbm.1, ...), custom_call_target="tpu_custom_call" | custom-call | tf_op jit(solution)/shard_map/pallas_call | solution.py:434
  22.1 1.7 %shard_map.113 = (f32[2,4]{1,0:T(2,128)}, f32[3,8,8,128]{3,2,1,0:T(8,128)}, f32[3,8,8,128]{3,2,1,0:T(8,128)}) custom-call(s32[1]{0:T(128)S(6)} %copy.12.accepted_ref, f32[2,4]{1,0:T(2,128)} %get-tuple-element.5.n_ref, f32[3,8,8,128]{3,2,1,0:T(8,128)} %v_ref.1, f32[3,8,8,128]{3,2,1,0:T(8,128)} %d_ref.1, f32[3,8,8,128]{3,2,1,0:T(8,128)} %get-tuple-element.6.r_ref), custom_call_target="tpu_custom_call" | custom-call | tf_op jit(solution)/shard_map/pallas_call | solution.py:456
